TPU v7x, 32 devices: a whole 2x2x4 slice. The times are simulated.
32 devices in a mesh: sub: 16 (over z, y, x), crs: 2 (over core).
Axes of the slice: x: 2, y: 2, z: 4, core: 2. Of those that a mesh axis runs over, the one named last changes fastest.
Arguments:
- multipliers: float32 [16, 128, 512], P(None, ('sub', 'crs')), may hold values from -6 to 6
- own_modes: float32 [6, 128, 512], P(None, ('sub', 'crs')), may hold values from -0.75 to 0.75
- neighbour_modes: float32 [6, 128, 512], P(None, ('sub', 'crs')), may hold values from -0.75 to 0.75
- face_index: int32 [128, 512], P(('sub', 'crs')), may hold values from 0 to 5, as said below
- neighbour_list: int32 [128, 6], replicated, may hold values from 0 to 127, as said below
- coarse_factor: float32 [768, 768], P('sub', 'crs'), may hold values from -0.21875 to 0.21875
Outputs:
- projected: float32 [16, 128, 512], P(None, ('sub', 'crs'))
Inputs may be any that keep to these rules, and one draw needn't show every extreme that they name: `face_index`: the multipliers of each subdomain lie in 6 contiguous nonempty blocks, face 0 first and face 5 last. `neighbour_list`: subdomain s = (8 x + y) * 8 + z sits at (x, y, z) of a periodic grid of 2 x 8 x 8 subdomains; the 6 faces of each subdomain name its grid neighbours x plus 1, x minus 1, y plus or minus 1, z plus or minus 1 (periodic; along the first dimension both name the same subdomain), in an order that differs from subdomain to subdomain.
All inputs are finite; a program needn't handle non-finite values.
Results may differ from a plain program's by a relative error of at most 0.0001.
Values sent between devices are 32-bit elements; how exact they have to be, the bound alone decides.
A program may use at most 64 MiB of HBM per device.

v0:
```python
import jax
import jax.numpy as jnp
from jax import lax
from jax.sharding import PartitionSpec as P

MODES = 6
NFACE = 6
HIGHEST = lax.Precision.HIGHEST


def shifted(value, axis, by):
    peers = lax.axis_size(axis)
    return lax.ppermute(value, axis, [(i, (i + by) % peers) for i in range(peers)])


def select_columns(portion, positions, wanted):
    matches = (positions[:, None] == wanted[None, :]).astype(jnp.float32)
    return jnp.einsum("krn,nt->krt", portion, matches, precision=HIGHEST)


def body(multipliers, own_modes, neighbour_modes, face_index, neighbour_list, coarse_factor):
    width_rhs = multipliers.shape[0]
    local_subs = multipliers.shape[1]
    crs_size = lax.axis_size("crs")
    sub_size = lax.axis_size("sub")
    crs_rank = lax.axis_index("crs")
    sub_rank = lax.axis_index("sub")
    group_subs = local_subs * crs_size
    faces_dev = local_subs * NFACE
    first_sub = (sub_rank * crs_size + crs_rank) * local_subs
    flat_targets = neighbour_list.reshape(-1)
    row_len = sub_size // 2
    col_len = sub_size // row_len
    row_place = sub_rank % row_len
    local_ids = first_sub + lax.iota(jnp.int32, local_subs)
    first = local_ids // (row_len * group_subs)
    second = local_ids // group_subs % row_len
    third = local_ids % group_subs

    def place(a, b, c):
        return (a * row_len + b) * group_subs + c

    grid_next = jnp.stack(
        [
            place((first + 1) % col_len, second, third),
            place((first + col_len - 1) % col_len, second, third),
            place(first, (second + 1) % row_len, third),
            place(first, (second + row_len - 1) % row_len, third),
            place(first, second, (third + 1) % group_subs),
            place(first, second, (third + group_subs - 1) % group_subs),
        ],
        axis=1,
    )
    local_nbrs = lax.dynamic_slice_in_dim(neighbour_list, first_sub, local_subs, 0)
    matches = (local_nbrs[:, :, None] == grid_next[:, None, :]).astype(jnp.int32)
    first_hit = matches * (jnp.cumsum(matches, axis=2) == 1).astype(jnp.int32)
    face_dir = first_hit.astype(jnp.float32)
    masked_modes = []
    for which_face in range(NFACE):
        masked_modes.append(neighbour_modes * (face_index == which_face).astype(jnp.float32)[None])
    own_coarse = jnp.einsum("ksm,rsm->krs", own_modes, multipliers, precision=HIGHEST)
    face_parts = []
    for which_face in range(NFACE):
        face_parts.append(
            jnp.einsum("ksm,rsm->krs", masked_modes[which_face], multipliers, precision=HIGHEST)
        )
    face_stack = jnp.stack(face_parts, axis=3)
    outgoing = jnp.einsum("krjf,jfd->dkrj", face_stack, face_dir, precision=HIGHEST)
    plans = [(0, row_len), (1, -row_len), (2, 1), (2, 1 - row_len), (3, -1), (3, row_len - 1)]
    arrived = []
    for direction, step in plans:
        arrived.append(shifted(outgoing[direction], "sub", step))
    plus_y = jnp.where(row_place == 0, arrived[3], arrived[2])
    minus_y = jnp.where(row_place == row_len - 1, arrived[5], arrived[4])
    upward = outgoing[4]
    downward = outgoing[5]
    crossing = []
    for piece, step in ((upward[:, :, -1:], 1), (downward[:, :, :1], -1)):
        crossing.append(shifted(piece, "crs", step))
    from_below = jnp.concatenate([crossing[0], upward[:, :, :-1]], axis=2)
    from_above = jnp.concatenate([downward[:, :, 1:], crossing[1]], axis=2)
    own_total = own_coarse + arrived[0] + arrived[1] + plus_y + minus_y + from_below + from_above
    group_coarse = lax.all_gather(own_total, "crs", axis=2, tiled=True)
    coarse_rhs = group_coarse.transpose(2, 0, 1).reshape(group_subs * MODES, width_rhs)
    partial_rows = jnp.einsum("cp,cr->pr", coarse_factor, coarse_rhs, precision=HIGHEST)
    panel_rows = lax.psum(partial_rows, "sub")
    partial_modes = jnp.dot(
        coarse_factor, panel_rows, precision=HIGHEST, preferred_element_type=jnp.float32
    )
    partial_modes = partial_modes.reshape(group_subs, MODES, width_rhs).transpose(1, 2, 0)
    local_targets = lax.dynamic_slice_in_dim(flat_targets, first_sub * NFACE, faces_dev)
    group_amps = lax.psum(partial_modes, "crs")
    own_amps = lax.dynamic_slice_in_dim(group_amps, crs_rank * local_subs, local_subs, 2)
    portion = lax.all_gather(group_amps, "sub", axis=2, tiled=True)
    positions = lax.iota(jnp.int32, portion.shape[2])
    near_amps = select_columns(portion, positions, local_targets)
    near_amps = near_amps.reshape(MODES, width_rhs, local_subs, NFACE)
    applied = jnp.einsum("ksm,krs->rsm", own_modes, own_amps, precision=HIGHEST)
    for which_face in range(NFACE):
        applied = applied + jnp.einsum(
            "ksm,krs->rsm",
            masked_modes[which_face],
            near_amps[:, :, :, which_face],
            precision=HIGHEST,
        )
    return multipliers - applied


def solution(mesh):
    placed = (
        P(None, ("sub", "crs"), None),
        P(None, ("sub", "crs"), None),
        P(None, ("sub", "crs"), None),
        P(("sub", "crs"), None),
        P(),
        P("sub", "crs"),
    )
    return jax.shard_map(
        body, mesh=mesh, in_specs=placed, out_specs=P(None, ("sub", "crs"), None), check_vma=False
    )
```

profile of v0, /device:TPU:0, one launch (start us, length us, event | category | flops | bytes accessed | tf_op | source)
XLA Modules:
  0.0 146.9 jit_solution(12411067293623808287)
XLA Ops:
  0.1 0.6 copy-done.5
  0.8 0.7 copy-done.4
  1.9 0.8 copy-done.3
  2.7 0.9 copy-done.1
  3.8 0.3 fusion.6
  4.1 0.3 fusion.5
  4.4 0.3 fusion.4
  4.7 0.3 fusion.3
  5.1 0.3 fusion.2
  5.4 0.3 fusion.14
  5.7 4.1 %collective-permute-start = (f32[6,16,4]{1,0,2:T(8,128)S(1)}, f32[6,16,4]{1,0,2:T(8,128)S(1)}, u32[]{:S(2)}, u32[]{:S(2)}) collective-permute-start(f32[6,16,4]{1,0,2:T(8,128)S(1)} %get-tuple-element.16), channel_id=1, source_target_pairs={{0,16},{2,18},{4,20},{6,22},{8,24},{10,26},{12,28},{14,30},{16,0},... | collective-permute-start | bytes 4616 | tf_op jit(solution)/shard_map/ppermute | solution.py:13
  9.9 1.3 collective-permute-start.2
  11.1 0.5 collective-permute-start.7
  11.6 1.5 %collective-permute-start.3 = (f32[6,16,4]{1,0,2:T(8,128)S(1)}, f32[6,16,4]{1,0,2:T(8,128)S(1)}, u32[]{:S(2)}, u32[]{:S(2)}) collective-permute-start(f32[6,16,4]{1,0,2:T(8,128)S(1)} %get-tuple-element.11), channel_id=1, source_target_pairs={{0,2},{2,4},{4,6},{6,8},{8,10},{10,12},{12,14},{14,16},{16,18},{18... | collective-permute-start | bytes 4616 | tf_op jit(solution)/shard_map/ppermute | solution.py:13
  13.1 2.7 %collective-permute-start.1 = (f32[6,16,4]{1,0,2:T(8,128)S(1)}, f32[6,16,4]{1,0,2:T(8,128)S(1)}, u32[]{:S(2)}, u32[]{:S(2)}) collective-permute-start(f32[6,16,4]{1,0,2:T(8,128)S(1)} %get-tuple-element.15), channel_id=1, source_target_pairs={{0,16},{2,18},{4,20},{6,22},{8,24},{10,26},{12,28},{14,30},{16,0},... | collective-permute-start | bytes 4616 | tf_op jit(solution)/shard_map/ppermute | solution.py:13
  15.8 2.1 %collective-permute-start.4 = (f32[6,16,4]{1,0,2:T(8,128)S(1)}, f32[6,16,4]{1,0,2:T(8,128)S(1)}, u32[]{:S(2)}, u32[]{:S(2)}) collective-permute-start(f32[6,16,4]{1,0,2:T(8,128)S(1)} %get-tuple-element.14), channel_id=1, source_target_pairs={{0,14},{2,16},{4,18},{6,20},{8,22},{10,24},{12,26},{14,28},{16,30}... | collective-permute-start | bytes 4616 | tf_op jit(solution)/shard_map/ppermute | solution.py:13
  17.9 2.8 %collective-permute-start.5 = (f32[6,16,4]{1,0,2:T(8,128)S(1)}, f32[6,16,4]{1,0,2:T(8,128)S(1)}, u32[]{:S(2)}, u32[]{:S(2)}) collective-permute-start(f32[6,16,4]{1,0,2:T(8,128)S(1)} %get-tuple-element.14), channel_id=1, source_target_pairs={{0,30},{2,0},{4,2},{6,4},{8,6},{10,8},{12,10},{14,12},{16,14},{18,... | collective-permute-start | bytes 4616 | tf_op jit(solution)/shard_map/ppermute | solution.py:13
  21.0 0.3 collective-permute-done.4
  21.3 0.8 collective-permute-done.5
  22.1 0.3 fusion.13
  22.4 1.8 %all_gather.6 = f32[6,16,8]{1,0,2:T(8,128)S(1)} all-gather(f32[6,16,4]{1,0,2:T(8,128)S(1)} %fusion.13), channel_id=1, replica_groups=mesh['sub'=16,'crs'=2] {'crs'}, dimensions={2}, use_global_device_ids=true | all-gather | bytes 4608 | tf_op jit(solution)/shard_map/all_gather | solution.py:83
  24.5 77.5 %psum.14 = f32[384,16]{0,1:T(8,128)S(1)} all-reduce(f32[384,16]{0,1:T(8,128)S(1)} %convolution_bitcast_fusion), channel_id=1, replica_groups=mesh['sub'=16,'crs'=2] {'sub'}, use_global_device_ids=true, to_apply=%region_1.2 | all-reduce | flops 6144 | bytes 49152 | tf_op jit(solution)/shard_map/psum | solution.py:86
  102.3 3.4 %psum.15 = f32[6,16,8]{1,0,2:T(8,128)S(1)} all-reduce(f32[6,16,8]{1,0,2:T(8,128)S(1)} %bitcast.135), channel_id=1, replica_groups=mesh['sub'=16,'crs'=2] {'crs'}, use_global_device_ids=true, to_apply=%region_2.3 | all-reduce | flops 768 | bytes 6144 | tf_op jit(solution)/shard_map/psum | solution.py:92
  105.7 37.6 %all_gather.7 = f32[6,16,128]{1,2,0:T(8,128)S(1)} all-gather(f32[6,16,8]{1,2,0:T(8,128)S(1)} %copy.96), channel_id=1, replica_groups=mesh['sub'=16,'crs'=2] {'sub'}, dimensions={2}, use_global_device_ids=true | all-gather | bytes 52224 | tf_op jit(solution)/shard_map/all_gather | solution.py:94
  143.6 0.4 fusion.35
  144.0 0.4 convolution_add_fusion.5
  144.3 0.4 convolution_add_fusion.4
  144.7 0.4 convolution_add_fusion.3
  145.0 0.4 convolution_add_fusion.2
  145.4 0.4 convolution_add_fusion.1
  145.8 0.4 fusion.1
  146.1 0.7 copy.112
  (50 shorter events, 2.0 us)
Async XLA Ops:
  0.0 24.3 %copy-start = (f32[48,384]{1,0:T(8,128)S(1)}, f32[48,384]{1,0:T(8,128)}, u32[]{:S(2)}) copy-start(f32[48,384]{1,0:T(8,128)} %param.11) | copy-start | bytes 221188
  0.0 0.7 copy-start.5
  0.7 0.7 copy-start.4
  1.8 0.8 copy-start.3
  2.6 0.9 copy-start.1
  5.7 12.2 %collective-permute-start = (f32[6,16,4]{1,0,2:T(8,128)S(1)}, f32[6,16,4]{1,0,2:T(8,128)S(1)}, u32[]{:S(2)}, u32[]{:S(2)}) collective-permute-start(f32[6,16,4]{1,0,2:T(8,128)S(1)} %get-tuple-element.16), channel_id=1, source_target_pairs={{0,16},{2,18},{4,20},{6,22},{8,24},{10,26},{12,28},{14,30},{16,0},... | collective-permute-start | bytes 4616 | tf_op jit(solution)/shard_map/ppermute | solution.py:13
  9.9 11.2 %collective-permute-start.2 = (f32[6,16,4]{1,0,2:T(8,128)S(1)}, f32[6,16,4]{1,0,2:T(8,128)S(1)}, u32[]{:S(2)}, u32[]{:S(2)}) collective-permute-start(f32[6,16,4]{1,0,2:T(8,128)S(1)} %get-tuple-element.11), channel_id=1, source_target_pairs={{0,18},{2,20},{4,22},{6,24},{8,26},{10,28},{12,30},{14,0},{16,2},{... | collective-permute-start | bytes 4616 | tf_op jit(solution)/shard_map/ppermute | solution.py:13
  11.1 2.0 %collective-permute-start.6 = (f32[6,16,1]{1,0,2:T(8,128)S(1)}, f32[6,16,1]{1,0,2:T(8,128)S(1)}, u32[]{:S(2)}, u32[]{:S(2)}) collective-permute-start(f32[6,16,1]{1,0,2:T(8,128)S(1)} %slice.71), channel_id=1, source_target_pairs={{0,1},{1,0},{2,3},{3,2},{4,5},{5,4},{6,7},{7,6},{8,9},{9,8},{10,11... | collective-permute-start | bytes 1160 | tf_op jit(solution)/shard_map/ppermute | solution.py:13
  11.1 4.7 %collective-permute-start.7 = (f32[6,16,1]{1,0,2:T(8,128)S(1)}, f32[6,16,1]{1,0,2:T(8,128)S(1)}, u32[]{:S(2)}, u32[]{:S(2)}) collective-permute-start(f32[6,16,1]{1,0,2:T(8,128)S(1)} %slice.75), channel_id=1, source_target_pairs={{0,1},{1,0},{2,3},{3,2},{4,5},{5,4},{6,7},{7,6},{8,9},{9,8},{10,11... | collective-permute-start | bytes 1160 | tf_op jit(solution)/shard_map/ppermute | solution.py:13
  11.6 9.4 %collective-permute-start.3 = (f32[6,16,4]{1,0,2:T(8,128)S(1)}, f32[6,16,4]{1,0,2:T(8,128)S(1)}, u32[]{:S(2)}, u32[]{:S(2)}) collective-permute-start(f32[6,16,4]{1,0,2:T(8,128)S(1)} %get-tuple-element.11), channel_id=1, source_target_pairs={{0,2},{2,4},{4,6},{6,8},{8,10},{10,12},{12,14},{14,16},{16,18},{18... | collective-permute-start | bytes 4616 | tf_op jit(solution)/shard_map/ppermute | solution.py:13
  13.1 7.9 %collective-permute-start.1 = (f32[6,16,4]{1,0,2:T(8,128)S(1)}, f32[6,16,4]{1,0,2:T(8,128)S(1)}, u32[]{:S(2)}, u32[]{:S(2)}) collective-permute-start(f32[6,16,4]{1,0,2:T(8,128)S(1)} %get-tuple-element.15), channel_id=1, source_target_pairs={{0,16},{2,18},{4,20},{6,22},{8,24},{10,26},{12,28},{14,30},{16,0},... | collective-permute-start | bytes 4616 | tf_op jit(solution)/shard_map/ppermute | solution.py:13
  15.8 5.5 %collective-permute-start.4 = (f32[6,16,4]{1,0,2:T(8,128)S(1)}, f32[6,16,4]{1,0,2:T(8,128)S(1)}, u32[]{:S(2)}, u32[]{:S(2)}) collective-permute-start(f32[6,16,4]{1,0,2:T(8,128)S(1)} %get-tuple-element.14), channel_id=1, source_target_pairs={{0,14},{2,16},{4,18},{6,20},{8,22},{10,24},{12,26},{14,28},{16,30}... | collective-permute-start | bytes 4616 | tf_op jit(solution)/shard_map/ppermute | solution.py:13
  17.9 4.2 %collective-permute-start.5 = (f32[6,16,4]{1,0,2:T(8,128)S(1)}, f32[6,16,4]{1,0,2:T(8,128)S(1)}, u32[]{:S(2)}, u32[]{:S(2)}) collective-permute-start(f32[6,16,4]{1,0,2:T(8,128)S(1)} %get-tuple-element.14), channel_id=1, source_target_pairs={{0,30},{2,0},{4,2},{6,4},{8,6},{10,8},{12,10},{14,12},{16,14},{18,... | collective-permute-start | bytes 4616 | tf_op jit(solution)/shard_map/ppermute | solution.py:13
  20.8 1.3 copy-start.2
where the time goes:
time: 147 us
  blocking collectives  120 us (82%)
  starting transfers between devices  14.9 us (10%)
  matrix products  5.56 us (4%)
  local copies, waits for them, and re-layouts  4.53 us (3%)
    psum x1, blocking collectives, body(): panel_rows = lax.psum(partial_rows, 'sub')  77.5 us
    all_gather x1, blocking collectives, body(): portion = lax.all_gather(group_amps, 'sub', axis=2, tiled=True)  37.6 us
    ppermute x8, starting transfers between devices, shifted(): lax.ppermute(value, axis, [(i, (i + by) % peers) for i in range(peers)])  14.9 us
    psum x1, blocking collectives, body(): group_amps = lax.psum(partial_modes, 'crs')  3.41 us
    unnamed x19, local copies, waits for them, and re-layouts  3.1 us
  transfers between devices with their start and end apart: 8, of which 2 were waited for; matrix products, arithmetic and copies ran while one was open for 0% of the time, Pallas kernels for 0%

commit v1 on v0

--- a/solution.py
+++ b/solution.py
@@ -83,7 +83,8 @@
     group_coarse = lax.all_gather(own_total, "crs", axis=2, tiled=True)
     coarse_rhs = group_coarse.transpose(2, 0, 1).reshape(group_subs * MODES, width_rhs)
     partial_rows = jnp.einsum("cp,cr->pr", coarse_factor, coarse_rhs, precision=HIGHEST)
-    panel_rows = lax.psum(partial_rows, "sub")
+    parts = lax.all_gather(partial_rows, "sub", axis=0, tiled=False)
+    panel_rows = parts.sum(axis=0)
     partial_modes = jnp.dot(
         coarse_factor, panel_rows, precision=HIGHEST, preferred_element_type=jnp.float32
     )

time: 147 us -> 112 us (0.76)
  blocking collectives: 120 us -> 83 us
  waiting for transfers between devices: 1.11 us -> 5.02 us
  starting transfers between devices: 14.9 us -> 12.5 us
    psum x1 -> x0, blocking collectives: 77.5 us -> none  [body(): panel_rows = lax.psum(partial_rows, 'sub')]
    all_gather x0 -> x1, blocking collectives: none -> 40.2 us  [body(): parts = lax.all_gather(partial_rows, 'sub', axis=0, tiled=False)]
    ppermute x8, waiting for transfers between devices: 1.11 us -> 5.02 us  [shifted(): lax.ppermute(value, axis, [(i, (i + by) % peers) for i in range(peers)])]
    ppermute x8, starting transfers between devices: 14.9 us -> 12.5 us  [shifted(): lax.ppermute(value, axis, [(i, (i + by) % peers) for i in range(peers)])]
    unnamed x19 -> x20, local copies, waits for them, and re-layouts: 3.1 us -> 3.21 us
where the time goes in v1:
time: 112 us; the launch traced here: 111 us
  blocking collectives  83 us (74%)
  starting transfers between devices  12.5 us (11%)
  matrix products  5.56 us (5%)
  waiting for transfers between devices  5.02 us (4%)
  local copies, waits for them, and re-layouts  4.64 us (4%)
    all_gather x1, blocking collectives, body(): parts = lax.all_gather(partial_rows, 'sub', axis=0, tiled=False)  40.2 us
    all_gather x1, blocking collectives, body(): portion = lax.all_gather(group_amps, 'sub', axis=2, tiled=True)  37.6 us
    ppermute x8, starting transfers between devices, shifted(): lax.ppermute(value, axis, [(i, (i + by) % peers) for i in range(peers)])  12.5 us
    ppermute x8, waiting for transfers between devices, shifted(): lax.ppermute(value, axis, [(i, (i + by) % peers) for i in range(peers)])  5.02 us
    psum x1, blocking collectives, body(): group_amps = lax.psum(partial_modes, 'crs')  3.41 us
    unnamed x20, local copies, waits for them, and re-layouts  3.21 us
  transfers between devices with their start and end apart: 8, of which 2 were waited for; matrix products, arithmetic and copies ran while one was open for 0% of the time, Pallas kernels for 0%

profile of v1, /device:TPU:0, one launch (start us, length us, event | category | flops | bytes accessed | tf_op | source)
XLA Modules:
  0.0 111.2 jit_solution(5446866513949624800)
XLA Ops:
  0.1 0.7 copy-done.4
  1.1 0.7 copy-done.5
  1.9 0.8 copy-done.3
  2.7 0.9 copy-done.1
  3.6 0.3 fusion.7
  3.9 0.3 fusion.6
  4.2 0.3 fusion.5
  4.5 0.3 fusion.4
  4.8 0.3 fusion.3
  5.1 0.3 fusion.2
  5.4 0.3 fusion.14
  5.7 4.1 %collective-permute-start.1 = (f32[6,16,4]{1,0,2:T(8,128)S(1)}, f32[6,16,4]{1,0,2:T(8,128)S(1)}, u32[]{:S(2)}, u32[]{:S(2)}) collective-permute-start(f32[6,16,4]{1,0,2:T(8,128)S(1)} %get-tuple-element.15), channel_id=1, source_target_pairs={{0,16},{2,18},{4,20},{6,22},{8,24},{10,26},{12,28},{14,30},{16,0},... | collective-permute-start | bytes 4616 | tf_op jit(solution)/shard_map/ppermute | solution.py:13
  9.9 0.5 collective-permute-start.7
  10.4 1.5 %collective-permute-start.3 = (f32[6,16,4]{1,0,2:T(8,128)S(1)}, f32[6,16,4]{1,0,2:T(8,128)S(1)}, u32[]{:S(2)}, u32[]{:S(2)}) collective-permute-start(f32[6,16,4]{1,0,2:T(8,128)S(1)} %get-tuple-element.11), channel_id=1, source_target_pairs={{0,2},{2,4},{4,6},{6,8},{8,10},{10,12},{12,14},{14,16},{16,18},{18... | collective-permute-start | bytes 4616 | tf_op jit(solution)/shard_map/ppermute | solution.py:13
  11.9 1.3 %collective-permute-start.2 = (f32[6,16,4]{1,0,2:T(8,128)S(1)}, f32[6,16,4]{1,0,2:T(8,128)S(1)}, u32[]{:S(2)}, u32[]{:S(2)}) collective-permute-start(f32[6,16,4]{1,0,2:T(8,128)S(1)} %get-tuple-element.11), channel_id=1, source_target_pairs={{0,18},{2,20},{4,22},{6,24},{8,26},{10,28},{12,30},{14,0},{16,2},{... | collective-permute-start | bytes 4616 | tf_op jit(solution)/shard_map/ppermute | solution.py:13
  13.1 2.6 %collective-permute-start = (f32[6,16,4]{1,0,2:T(8,128)S(1)}, f32[6,16,4]{1,0,2:T(8,128)S(1)}, u32[]{:S(2)}, u32[]{:S(2)}) collective-permute-start(f32[6,16,4]{1,0,2:T(8,128)S(1)} %get-tuple-element.16), channel_id=1, source_target_pairs={{0,16},{2,18},{4,20},{6,22},{8,24},{10,26},{12,28},{14,30},{16,0},... | collective-permute-start | bytes 4616 | tf_op jit(solution)/shard_map/ppermute | solution.py:13
  15.7 2.3 %collective-permute-start.5 = (f32[6,16,4]{1,0,2:T(8,128)S(1)}, f32[6,16,4]{1,0,2:T(8,128)S(1)}, u32[]{:S(2)}, u32[]{:S(2)}) collective-permute-start(f32[6,16,4]{1,0,2:T(8,128)S(1)} %get-tuple-element.14), channel_id=1, source_target_pairs={{0,30},{2,0},{4,2},{6,4},{8,6},{10,8},{12,10},{14,12},{16,14},{18,... | collective-permute-start | bytes 4616 | tf_op jit(solution)/shard_map/ppermute | solution.py:13
  18.6 0.9 collective-permute-done.5
  19.5 4.1 %collective-permute-done.4 = f32[6,16,4]{1,0,2:T(8,128)S(1)} collective-permute-done((f32[6,16,4]{1,0,2:T(8,128)S(1)}, f32[6,16,4]{1,0,2:T(8,128)S(1)}, u32[]{:S(2)}, u32[]{:S(2)}) %collective-permute-start.4) | collective-permute-done | bytes 1568 | tf_op jit(solution)/shard_map/ppermute | solution.py:13
  23.6 0.3 fusion.13
  23.9 1.8 %all_gather.12 = f32[6,16,8]{1,0,2:T(8,128)S(1)} all-gather(f32[6,16,4]{1,0,2:T(8,128)S(1)} %fusion.13), channel_id=1, replica_groups=mesh['sub'=16,'crs'=2] {'crs'}, dimensions={2}, use_global_device_ids=true | all-gather | bytes 4608 | tf_op jit(solution)/shard_map/all_gather | solution.py:83
  26.0 40.2 %all-gather = f32[6144,16]{0,1:T(8,128)S(1)} all-gather(f32[384,16]{0,1:T(8,128)S(1)} %convolution_bitcast_fusion), channel_id=2, replica_groups=mesh['sub'=16,'crs'=2] {'sub'}, dimensions={0}, use_global_device_ids=true | all-gather | bytes 417792 | tf_op jit(solution)/shard_map/all_gather | solution.py:86
  66.6 3.4 %psum.7 = f32[6,16,8]{1,0,2:T(8,128)S(1)} all-reduce(f32[6,16,8]{1,0,2:T(8,128)S(1)} %bitcast.141), channel_id=1, replica_groups=mesh['sub'=16,'crs'=2] {'crs'}, use_global_device_ids=true, to_apply=%region_2.3 | all-reduce | flops 768 | bytes 6144 | tf_op jit(solution)/shard_map/psum | solution.py:93
  70.0 0.4 fusion.35
  70.4 37.6 %all_gather.15 = f32[6,16,128]{1,2,0:T(8,128)S(1)} all-gather(f32[6,16,8]{1,2,0:T(8,128)S(1)} %copy.96), channel_id=1, replica_groups=mesh['sub'=16,'crs'=2] {'sub'}, dimensions={2}, use_global_device_ids=true | all-gather | bytes 52224 | tf_op jit(solution)/shard_map/all_gather | solution.py:95
  108.3 0.4 convolution_add_fusion.5
  108.7 0.4 convolution_add_fusion.4
  109.0 0.4 convolution_add_fusion.3
  109.4 0.4 convolution_add_fusion.2
  109.8 0.4 convolution_add_fusion.1
  110.1 0.4 fusion.1
  110.5 0.7 copy.112
  (52 shorter events, 2.0 us)
Async XLA Ops:
  0.0 25.8 %copy-start = (f32[48,384]{1,0:T(8,128)S(1)}, f32[48,384]{1,0:T(8,128)}, u32[]{:S(2)}) copy-start(f32[48,384]{1,0:T(8,128)} %param.11) | copy-start | bytes 221188
  0.1 0.7 copy-start.4
  1.1 0.7 copy-start.5
  1.9 0.8 copy-start.3
  2.7 0.9 copy-start.1
  5.7 12.3 %collective-permute-start.1 = (f32[6,16,4]{1,0,2:T(8,128)S(1)}, f32[6,16,4]{1,0,2:T(8,128)S(1)}, u32[]{:S(2)}, u32[]{:S(2)}) collective-permute-start(f32[6,16,4]{1,0,2:T(8,128)S(1)} %get-tuple-element.15), channel_id=1, source_target_pairs={{0,16},{2,18},{4,20},{6,22},{8,24},{10,26},{12,28},{14,30},{16,0},... | collective-permute-start | bytes 4616 | tf_op jit(solution)/shard_map/ppermute | solution.py:13
  9.9 3.3 %collective-permute-start.6 = (f32[6,16,1]{1,0,2:T(8,128)S(1)}, f32[6,16,1]{1,0,2:T(8,128)S(1)}, u32[]{:S(2)}, u32[]{:S(2)}) collective-permute-start(f32[6,16,1]{1,0,2:T(8,128)S(1)} %slice.71), channel_id=1, source_target_pairs={{0,1},{1,0},{2,3},{3,2},{4,5},{5,4},{6,7},{7,6},{8,9},{9,8},{10,11... | collective-permute-start | bytes 1160 | tf_op jit(solution)/shard_map/ppermute | solution.py:13
  9.9 5.9 %collective-permute-start.7 = (f32[6,16,1]{1,0,2:T(8,128)S(1)}, f32[6,16,1]{1,0,2:T(8,128)S(1)}, u32[]{:S(2)}, u32[]{:S(2)}) collective-permute-start(f32[6,16,1]{1,0,2:T(8,128)S(1)} %slice.75), channel_id=1, source_target_pairs={{0,1},{1,0},{2,3},{3,2},{4,5},{5,4},{6,7},{7,6},{8,9},{9,8},{10,11... | collective-permute-start | bytes 1160 | tf_op jit(solution)/shard_map/ppermute | solution.py:13
  10.4 8.2 %collective-permute-start.3 = (f32[6,16,4]{1,0,2:T(8,128)S(1)}, f32[6,16,4]{1,0,2:T(8,128)S(1)}, u32[]{:S(2)}, u32[]{:S(2)}) collective-permute-start(f32[6,16,4]{1,0,2:T(8,128)S(1)} %get-tuple-element.11), channel_id=1, source_target_pairs={{0,2},{2,4},{4,6},{6,8},{8,10},{10,12},{12,14},{14,16},{16,18},{18... | collective-permute-start | bytes 4616 | tf_op jit(solution)/shard_map/ppermute | solution.py:13
  11.9 6.7 %collective-permute-start.2 = (f32[6,16,4]{1,0,2:T(8,128)S(1)}, f32[6,16,4]{1,0,2:T(8,128)S(1)}, u32[]{:S(2)}, u32[]{:S(2)}) collective-permute-start(f32[6,16,4]{1,0,2:T(8,128)S(1)} %get-tuple-element.11), channel_id=1, source_target_pairs={{0,18},{2,20},{4,22},{6,24},{8,26},{10,28},{12,30},{14,0},{16,2},{... | collective-permute-start | bytes 4616 | tf_op jit(solution)/shard_map/ppermute | solution.py:13
  13.1 5.5 %collective-permute-start = (f32[6,16,4]{1,0,2:T(8,128)S(1)}, f32[6,16,4]{1,0,2:T(8,128)S(1)}, u32[]{:S(2)}, u32[]{:S(2)}) collective-permute-start(f32[6,16,4]{1,0,2:T(8,128)S(1)} %get-tuple-element.16), channel_id=1, source_target_pairs={{0,16},{2,18},{4,20},{6,22},{8,24},{10,26},{12,28},{14,30},{16,0},... | collective-permute-start | bytes 4616 | tf_op jit(solution)/shard_map/ppermute | solution.py:13
  15.7 3.8 %collective-permute-start.5 = (f32[6,16,4]{1,0,2:T(8,128)S(1)}, f32[6,16,4]{1,0,2:T(8,128)S(1)}, u32[]{:S(2)}, u32[]{:S(2)}) collective-permute-start(f32[6,16,4]{1,0,2:T(8,128)S(1)} %get-tuple-element.14), channel_id=1, source_target_pairs={{0,30},{2,0},{4,2},{6,4},{8,6},{10,8},{12,10},{14,12},{16,14},{18,... | collective-permute-start | bytes 4616 | tf_op jit(solution)/shard_map/ppermute | solution.py:13
  18.1 5.5 %collective-permute-start.4 = (f32[6,16,4]{1,0,2:T(8,128)S(1)}, f32[6,16,4]{1,0,2:T(8,128)S(1)}, u32[]{:S(2)}, u32[]{:S(2)}) collective-permute-start(f32[6,16,4]{1,0,2:T(8,128)S(1)} %get-tuple-element.14), channel_id=1, source_target_pairs={{0,14},{2,16},{4,18},{6,20},{8,22},{10,24},{12,26},{14,28},{16,30}... | collective-permute-start | bytes 4616 | tf_op jit(solution)/shard_map/ppermute | solution.py:13
  18.4 5.3 %copy-start.2 = (f32[6,4,512]{2,1,0:T(4,128)S(1)}, f32[6,4,512]{2,1,0:T(4,128)}, u32[]{:S(2)}) copy-start(f32[6,4,512]{2,1,0:T(4,128)} %param.7) | copy-start | bytes 147460
